TPU v7x, 256 devices: a 8x8x2 block of a 8x8x16 slice. The times are simulated.
256 devices in a mesh: groups: 2 (over z), attn: 16 (over y, core), expert: 8 (over x).
Axes of the slice: x: 8, y: 8, z: 2, core: 2. Of those that a mesh axis runs over, the one named last changes fastest.
The devices are a block of a 8x8x16 slice.
Arguments:
- tokens: bfloat16 [4096, 4096], P(('groups', 'attn'), 'expert'), parts along dimension 0, may hold values from -6 to 6
- expert_ids: int32 [4096, 8], P(('groups', 'attn')), parts along dimension 0, may hold values from 0 to 63, all different within a row; in each aligned block of 128 rows (0 to 127, 128 to 255, ...) at most 48 rows name the same one
- gate_weight: bfloat16 [4096, 8], P(('groups', 'attn')), parts along dimension 0, may hold values from 0.049804688 to 0.29882812
- w_gate: bfloat16 [64, 4096, 768], P('attn', 'expert'), may hold values from -0.09375 to 0.09375
- w_up: bfloat16 [64, 4096, 768], P('attn', 'expert'), may hold values from -0.09375 to 0.09375
- w_down: bfloat16 [64, 768, 4096], P('attn', None, 'expert'), may hold values from -0.21875 to 0.21875
- query: bfloat16 [512, 64, 128], P(('groups', 'attn', 'expert')), parts along dimension 0, may hold values from -100 to 100
- cache_k: bfloat16 [512, 768, 4, 128], P(('groups', 'attn', 'expert')), parts along dimension 0, may hold values from -6 to 6
- cache_v: bfloat16 [512, 768, 4, 128], P(('groups', 'attn', 'expert')), parts along dimension 0, may hold values from -6 to 6
- lengths: int32 [512], P(('groups', 'attn', 'expert')), parts along dimension 0, may hold values from 2 to 768, as said below
Outputs:
- moe_out: bfloat16 [4096, 4096], P(('groups', 'attn'), 'expert'), parts along dimension 0
- attn_out: bfloat16 [512, 8192], P(('groups', 'attn', 'expert')), parts along dimension 0
There are 2 independent parts, one for each index of `groups`. A program takes and returns all parts, laid end to end along the dimension named above; an argument that names none is the same for every part. Nothing has to cross between parts.
Inputs may be any that keep to these rules, and one draw needn't show every extreme that they name: `expert_ids`: each row names 8 different experts. In the rows of one index of attn (aligned blocks of 128 rows) no expert is named by more than 48 rows, and in some block some expert by exactly 48. `lengths`: some sequence has all 768 positions live.
All inputs are finite; a program needn't handle non-finite values.
Results may differ from a plain program's by a relative error of at most 0.025.
Values may be sent and summed in bfloat16 or wider, within the bound.
No kernel may reach another device: no remote copies, remote signals or barrier semaphores. Data moves between devices by JAX's collectives and lax.ppermute only.
A program may use at most 64 MiB of HBM per device.

v0:
```python
import jax
import jax.numpy as jnp
from jax import lax
from jax.sharding import PartitionSpec as P


def laid_out(tiles, dim):
    dims = list(tiles.shape[1:])
    dims[dim] *= tiles.shape[0]
    return jnp.moveaxis(tiles, 0, dim).reshape(dims)


def copy_for_each(shard, axis):
    count = lax.axis_size(axis)
    return lax.all_to_all(
        jnp.broadcast_to(shard[None], (count, *shard.shape)), axis, 0, 0, tiled=True
    )


def gather_directly(shard, axis, dim):
    return laid_out(copy_for_each(shard, axis), dim)


def member_table(expert_ids, experts):
    wanted = jnp.arange(experts, dtype=jnp.int32)
    return jnp.any(expert_ids[:, :, None] == wanted[None, None, :], axis=1).astype(jnp.int32)


def pad_rows(values):
    feat_width = values.shape[-1]
    flat_rows = values.reshape(-1, feat_width)
    return jnp.concatenate([flat_rows, jnp.zeros((1, feat_width), values.dtype)], axis=0)


def return_slots(results, starts_in, kept_in, slot_count):
    local_experts = results.shape[0]
    capacity = results.shape[1]
    slot_ids = jnp.arange(slot_count, dtype=jnp.int32)[None, None, :]
    column = jnp.arange(local_experts, dtype=jnp.int32)[None, :, None]
    row_index = column * capacity + starts_in[:, :, None] + slot_ids
    row_index = jnp.where(slot_ids < kept_in[:, :, None], row_index, local_experts * capacity)
    return pad_rows(results)[row_index]


def grouped_attention(query, cache_k, cache_v, lengths):
    seq_count, head_total, head_size = query.shape
    context = cache_k.shape[1]
    kv_count = cache_k.shape[2]
    grouped = query.reshape(seq_count, kv_count, head_total // kv_count, head_size)
    scores = jnp.einsum(
        "skgd,slkd->skgl", grouped, cache_k, preferred_element_type=jnp.float32
    ) * head_size ** (-0.5)
    live_mask = (
        lax.broadcasted_iota(jnp.int32, (seq_count, 1, 1, context), 3)
        < lengths[:, None, None, None]
    )
    masked = jnp.where(live_mask, scores, -jnp.inf)
    row_peak = jnp.max(masked, axis=3, keepdims=True)
    weighted = jnp.exp(masked - row_peak)
    denominator = jnp.sum(weighted, axis=3, keepdims=True)
    prob_bf = (weighted / denominator).astype(jnp.bfloat16)
    attended = jnp.einsum("skgl,slkd->skgd", prob_bf, cache_v, preferred_element_type=jnp.float32)
    return attended.reshape(seq_count, head_total * head_size).astype(jnp.bfloat16)


def body(tokens, expert_ids, gate_weight, w_gate, w_up, w_down, query, cache_k, cache_v, lengths):
    tok_rows, feat_width = tokens.shape
    top_count = expert_ids.shape[1]
    local_experts = w_gate.shape[0]
    ffn_width = w_gate.shape[2]
    attn_count = lax.axis_size("attn")
    experts = local_experts * attn_count
    capacity = tok_rows * top_count // local_experts
    slot_count = min(tok_rows, 3 * tok_rows * top_count // experts)
    member = member_table(expert_ids, experts)
    local_rank = jnp.cumsum(member, axis=0, dtype=jnp.int32) - member
    whole_ids = None
    whole_tokens, whole_ids, whole_gates = (
        gather_directly(tokens, "attn", 0),
        gather_directly(expert_ids, "attn", 0),
        gather_directly(gate_weight, "attn", 0),
    )
    all_rows = whole_tokens.shape[0]
    whole_member = member_table(whole_ids, experts)
    all_counts = jnp.sum(
        whole_member.reshape(attn_count, tok_rows, experts), axis=1, dtype=jnp.int32
    )
    src_offsets = jnp.cumsum(all_counts, axis=0, dtype=jnp.int32) - all_counts
    src_kept = jnp.clip(capacity - src_offsets, 0, all_counts)
    my_index = lax.axis_index("attn")
    offsets = lax.dynamic_index_in_dim(src_offsets, my_index, 0, keepdims=False)
    position = offsets[None, :] + local_rank
    starts_in = lax.dynamic_slice_in_dim(src_offsets, my_index * local_experts, local_experts, 1)
    kept_in = lax.dynamic_slice_in_dim(src_kept, my_index * local_experts, local_experts, 1)
    my_member = lax.dynamic_slice_in_dim(whole_member, my_index * local_experts, local_experts, 1)
    queue_place = jnp.cumsum(my_member, axis=0, dtype=jnp.int32) - my_member
    pack_target = jnp.where(
        (my_member > 0) & (queue_place < capacity),
        jnp.arange(local_experts, dtype=jnp.int32)[None, :] * capacity + queue_place,
        local_experts * capacity,
    )
    holders = jnp.broadcast_to(
        jnp.arange(all_rows, dtype=jnp.int32)[:, None], (all_rows, local_experts)
    )
    pack_index = (
        jnp.full((local_experts * capacity,), all_rows, jnp.int32)
        .at[pack_target.reshape(-1)]
        .set(holders.reshape(-1), mode="drop")
    )
    packed = pad_rows(whole_tokens)[pack_index].reshape(local_experts, capacity, feat_width)
    gate_part = jnp.einsum("jrd,jdf->jrf", packed, w_gate, preferred_element_type=jnp.float32)
    up_part = jnp.einsum("jrd,jdf->jrf", packed, w_up, preferred_element_type=jnp.float32)
    both_parts = jnp.concatenate([gate_part, up_part], axis=2)
    row_sums = lax.psum_scatter(
        both_parts.astype(jnp.bfloat16), "expert", scatter_dimension=1, tiled=True
    ).astype(jnp.float32)
    hidden_share = (jax.nn.silu(row_sums[:, :, :ffn_width]) * row_sums[:, :, ffn_width:]).astype(
        jnp.bfloat16
    )
    hidden = gather_directly(hidden_share, "expert", 1)
    results = jnp.einsum("jrf,jfd->jrd", hidden, w_down, preferred_element_type=jnp.float32).astype(
        jnp.bfloat16
    )
    back_rows = return_slots(results, starts_in, kept_in, slot_count)
    returned = lax.all_to_all(back_rows, "attn", split_axis=0, concat_axis=0, tiled=True)
    slot_of = jnp.take_along_axis(local_rank, expert_ids, axis=1)
    place_of = jnp.take_along_axis(position, expert_ids, axis=1)
    keep_mask = place_of < capacity
    picked = returned.reshape(experts * slot_count, feat_width)[expert_ids * slot_count + slot_of]
    factor = jnp.where(keep_mask, gate_weight.astype(jnp.float32), 0.0)
    moe_out = jnp.sum(factor[:, :, None] * picked.astype(jnp.float32), axis=1).astype(jnp.bfloat16)
    attn_out = grouped_attention(query, cache_k, cache_v, lengths)
    return (moe_out, attn_out)


def solution(mesh):
    return jax.shard_map(
        body,
        mesh=mesh,
        in_specs=(
            P(("groups", "attn"), "expert"),
            P(("groups", "attn"), None),
            P(("groups", "attn"), None),
            P("attn", "expert", None),
            P("attn", "expert", None),
            P("attn", None, "expert"),
            P(("groups", "attn", "expert"), None, None),
            P(("groups", "attn", "expert"), None, None, None),
            P(("groups", "attn", "expert"), None, None, None),
            P(("groups", "attn", "expert")),
        ),
        out_specs=(P(("groups", "attn"), "expert"), P(("groups", "attn", "expert"), None)),
        check_vma=False,
    )
```

profile of v0, /device:TPU:513, one launch (start us, length us, event | category | flops | bytes accessed | tf_op | source)
XLA Modules:
  0.0 318.8 jit_solution(7994495979518382753)
XLA Ops:
  8.0 30.9 %all_to_all.20 = s32[16,128,8]{1,2,0:T(8,128)S(1)} all-to-all(s32[16,128,8]{1,2,0:T(8,128)S(1)} %broadcast_in_dim.36), channel_id=1, replica_groups=mesh['groups'=2,'attn'=16,'expert'=8] {'attn'}, dimensions={0} | all-to-all | bytes 131072 | tf_op jit(solution)/shard_map/all_to_all | solution.py:15
  38.9 2.5 broadcast_in_dim.39
  41.4 4.5 %all-to-all-start.1 = ((bf16[16,128,512]{2,1,0:T(8,128)(2,1)}), bf16[16,128,512]{2,1,0:T(8,128)(2,1)}, u32[]{:S(2)}, u32[]{:S(2)}) async-start(bf16[16,128,512]{2,1,0:T(8,128)(2,1)} %broadcast_in_dim.39), calls=%async_computation.1 | async-start | bytes 4194304 | tf_op jit(solution)/shard_map/all_to_all | solution.py:15
  47.0 1.8 reshape.197
  51.2 1.2 reduce-window.6
  53.8 1.3 copy.130
  55.2 2.0 reshape.148
  57.2 30.4 %scatter_custom_fusion = s32[1024]{0:T(1024)S(1)} fusion(s32[8192]{0:T(1024)S(1)} %bitcast.73, s32[8192]{0:T(1024)S(1)} %reshape.197, s32[]{:T(128)} %constant.35.clone.1), kind=kCustom, calls=%fused_computation.58 | custom fusion | bytes 4100 | tf_op jit(solution)/shard_map/scatter | solution.py:108
  87.6 7.5 %all-to-all-done.1 = bf16[16,128,512]{2,1,0:T(8,128)(2,1)} async-done(((bf16[16,128,512]{2,1,0:T(8,128)(2,1)}), bf16[16,128,512]{2,1,0:T(8,128)(2,1)}, u32[]{:S(2)}, u32[]{:S(2)}) %all-to-all-start.1) | async-done | bytes 2097184 | tf_op jit(solution)/shard_map/all_to_all | solution.py:15
  95.2 3.1 concatenate.10
  98.3 7.0 %gather_fusion = bf16[1024,512]{1,0:T(8,128)(2,1)} fusion(bf16[2049,512]{1,0:T(8,128)(2,1)} %concatenate.10, s32[1024]{0:T(1024)S(1)} %fusion.22), kind=kCustom, calls=%fused_computation.2 | custom fusion | bytes 2101248 | tf_op jit(solution)/shard_map/gather | solution.py:110
  105.3 2.4 convolution_convert_fusion
  108.8 1.9 pad_maximum_fusion
  110.8 45.1 %reduce-scatter.2.cloned.1.call-done = bf16[4,32,1536]{2,1,0:T(8,128)(2,1)} async-done(((bf16[4,256,1536]{2,1,0:T(8,128)(2,1)}), bf16[4,32,1536]{2,1,0:T(8,128)(2,1)}) %reduce-scatter.2.cloned.1.call-update) | async-done | bytes 393232 | tf_op jit(solution)/shard_map/reduce_scatter | solution.py:114
  155.9 1.1 convert_element_type.45
  157.1 1.3 broadcast_in_dim.48
  158.4 5.5 %all-to-all-start.2 = ((bf16[8,4,32,768]{3,2,1,0:T(8,128)(2,1)}), bf16[8,4,32,768]{3,2,1,0:T(8,128)(2,1)}, u32[]{:S(2)}, u32[]{:S(2)}) async-start(bf16[8,4,32,768]{3,2,1,0:T(8,128)(2,1)} %broadcast_in_dim.48), calls=%async_computation.3 | async-start | bytes 3145728 | tf_op jit(solution)/shard_map/all_to_all | solution.py:15
  164.0 1.9 copy.138
  165.9 2.2 reduce_sum.27
  168.5 33.4 %all-to-all-done.2 = bf16[8,4,32,768]{3,2,1,0:T(8,128)(2,1)} async-done(((bf16[8,4,32,768]{3,2,1,0:T(8,128)(2,1)}), bf16[8,4,32,768]{3,2,1,0:T(8,128)(2,1)}, u32[]{:S(2)}, u32[]{:S(2)}) %all-to-all-start.2) | async-done | bytes 1572896 | tf_op jit(solution)/shard_map/all_to_all | solution.py:15
  201.9 1.7 copy.131
  205.2 1.1 concatenate.12
  206.3 14.7 %gather_fusion.1 = bf16[3072,512]{1,0:T(8,128)(2,1)} fusion(bf16[1025,512]{1,0:T(8,128)(2,1)} %concatenate.12, s32[3072]{0:T(1024)S(1)} %broadcast_clamp_fusion), kind=kCustom, calls=%fused_computation.3 | custom fusion | bytes 6303744 | tf_op jit(solution)/shard_map/gather | solution.py:42
  221.0 9.9 %all-to-all-start.3 = ((bf16[16,4,48,512]{3,2,1,0:T(8,128)(2,1)}), bf16[16,4,48,512]{3,2,1,0:T(8,128)(2,1)}, u32[]{:S(2)}, u32[]{:S(2)}) async-start(bf16[16,4,48,512]{3,2,1,0:T(8,128)(2,1)} %bitcast.65), calls=%async_computation.4 | async-start | bytes 6291456 | tf_op jit(solution)/shard_map/all_to_all | solution.py:125
  232.1 1.9 fusion.12
  234.9 2.5 fusion.15
  237.4 1.4 copy.157
  239.6 7.1 %gather_fusion.3 = s32[1024]{0:T(1024)S(1)} fusion(s32[128,64]{1,0:T(8,128)S(1)} %get-tuple-element.3, s32[1024]{0:T(1024)S(1)} %reshape.217), kind=kCustom, calls=%fused_computation.clone | custom fusion | bytes 16384 | tf_op jit(solution)/shard_map/jit(take_along_axis)/gather | solution.py:127
  246.7 7.1 %gather_fusion.4 = s32[1024]{0:T(1024)S(1)} fusion(s32[128,64]{1,0:T(8,128)S(1)} %get-tuple-element.4, s32[1024]{0:T(1024)S(1)} %reshape.217), kind=kCustom, calls=%fused_computation.1.clone | custom fusion | bytes 16384 | tf_op jit(solution)/shard_map/jit(take_along_axis)/gather | solution.py:126
  254.5 47.5 %all-to-all-done.3 = bf16[16,4,48,512]{3,2,1,0:T(8,128)(2,1)} async-done(((bf16[16,4,48,512]{3,2,1,0:T(8,128)(2,1)}), bf16[16,4,48,512]{3,2,1,0:T(8,128)(2,1)}, u32[]{:S(2)}, u32[]{:S(2)}) %all-to-all-start.3) | async-done | bytes 3145760 | tf_op jit(solution)/shard_map/all_to_all | solution.py:125
  301.9 7.4 %gather_fusion.2 = bf16[1024,512]{1,0:T(8,128)(2,1)} fusion(bf16[3072,512]{1,0:T(8,128)(2,1)} %bitcast.12, s32[1024]{0:T(1024)S(1)} %broadcast_clamp_fusion.1), kind=kCustom, calls=%fused_computation.4 | custom fusion | bytes 2101248 | tf_op jit(solution)/shard_map/gather | solution.py:129
  309.3 2.6 fusion.2
  (64 shorter events, 12.7 us)
Async XLA Ops:
  7.2 98.1 %copy-start = (bf16[4,512,768]{2,1,0:T(8,128)(2,1)S(1)}, bf16[4,512,768]{2,1,0:T(8,128)(2,1)}, u32[]{:S(2)}) copy-start(bf16[4,512,768]{2,1,0:T(8,128)(2,1)} %param.16) | copy-start | bytes 9437188
  41.4 53.8 %all-to-all-start.1 = ((bf16[16,128,512]{2,1,0:T(8,128)(2,1)}), bf16[16,128,512]{2,1,0:T(8,128)(2,1)}, u32[]{:S(2)}, u32[]{:S(2)}) async-start(bf16[16,128,512]{2,1,0:T(8,128)(2,1)} %broadcast_in_dim.39), calls=%async_computation.1 | async-start | bytes 4194304 | tf_op jit(solution)/shard_map/all_to_all | solution.py:15
  45.9 110.0 %reduce-scatter.2.cloned.1.call-start = ((), (), s32[]{:S(2)}) async-start(), calls=%async_computation.5 | async-start | bytes 3538944 | tf_op jit(solution)/shard_map/reduce_scatter | solution.py:114
  50.4 0.8 copy-start.3
  105.3 2.4 copy-start.1
  105.3 2.5 copy-start.2
  158.4 43.5 %all-to-all-start.2 = ((bf16[8,4,32,768]{3,2,1,0:T(8,128)(2,1)}), bf16[8,4,32,768]{3,2,1,0:T(8,128)(2,1)}, u32[]{:S(2)}, u32[]{:S(2)}) async-start(bf16[8,4,32,768]{3,2,1,0:T(8,128)(2,1)} %broadcast_in_dim.48), calls=%async_computation.3 | async-start | bytes 3145728 | tf_op jit(solution)/shard_map/all_to_all | solution.py:15
  201.9 2.4 copy-start.8
  221.0 9.9 %copy-start.5 = (s32[128,8]{0,1:T(8,128)S(1)}, s32[128,8]{0,1:T(8,128)}, u32[]{:S(2)}) copy-start(s32[128,8]{0,1:T(8,128)} %param.13) | copy-start | bytes 12292
  221.0 11.1 %copy-start.7 = (s32[2]{0:T(128)S(1)}, s32[2]{0:T(128)}, u32[]{:S(2)}) copy-start(s32[2]{0:T(128)} %param.21) | copy-start | bytes 28
  221.0 80.9 %all-to-all-start.3 = ((bf16[16,4,48,512]{3,2,1,0:T(8,128)(2,1)}), bf16[16,4,48,512]{3,2,1,0:T(8,128)(2,1)}, u32[]{:S(2)}, u32[]{:S(2)}) async-start(bf16[16,4,48,512]{3,2,1,0:T(8,128)(2,1)} %bitcast.65), calls=%async_computation.4 | async-start | bytes 6291456 | tf_op jit(solution)/shard_map/all_to_all | solution.py:125
  231.0 1.1 copy-start.4
  246.7 7.6 %copy-start.6 = (bf16[128,8]{0,1:T(8,128)(2,1)S(1)}, bf16[128,8]{0,1:T(8,128)(2,1)}, u32[]{:S(2)}) copy-start(bf16[128,8]{0,1:T(8,128)(2,1)} %param.14) | copy-start | bytes 6148
Sparse Core Ops, SparseCore 0:
  110.9 44.9 reduce-scatter.1
where the time goes:
time: 320 us; the launch traced here: 319 us
  waiting for transfers between devices  134 us (42%)
  local copies, waits for them, and re-layouts  96.5 us (30%)
  blocking collectives  30.9 us (10%)
  starting transfers between devices  20 us (6%)
  other arithmetic  14.7 us (5%)
  between operations  14.3 us (4%)
  matrix products  8.71 us (3%)
    all_to_all x1, waiting for transfers between devices, body(): lax.all_to_all(back_rows, 'attn', split_axis=0, concat_axis=0, tiled=True)  47.5 us
    reduce_scatter x1, waiting for transfers between devices, body(): lax.psum_scatter(both_parts.astype(jnp.bfloat16), 'expert', scatter_dimen...  45.1 us
    all_to_all x2, waiting for transfers between devices, copy_for_each(): lax.all_to_all(jnp.broadcast_to(shard[None], (count, *shard.shape)), axis...  40.9 us
    all_to_all x1, blocking collectives, copy_for_each(): lax.all_to_all(jnp.broadcast_to(shard[None], (count, *shard.shape)), axis...  30.9 us
    scatter x1, local copies, waits for them, and re-layouts, body(): pack_index = jnp.full((local_experts * capacity,), all_rows, jnp.int32).a...  30.4 us
    gather x1, local copies, waits for them, and re-layouts, return_slots(): return pad_rows(results)[row_index]  14.7 us
    all_to_all x2, starting transfers between devices, copy_for_each(): lax.all_to_all(jnp.broadcast_to(shard[None], (count, *shard.shape)), axis...  10.1 us
    all_to_all x1, starting transfers between devices, body(): lax.all_to_all(back_rows, 'attn', split_axis=0, concat_axis=0, tiled=True)  9.88 us
  transfers between devices with their start and end apart: 4, of which 4 were waited for; matrix products, arithmetic and copies ran while one was open for 22% of the time, Pallas kernels for 0%

commit v1 on v0

--- a/solution.py
+++ b/solution.py
@@ -2,6 +2,17 @@
 import jax.numpy as jnp
 from jax import lax
 from jax.sharding import PartitionSpec as P
+
+
+def cut_along(shard, dim, devices):
+    before, after = (shard.shape[:dim], shard.shape[dim + 1 :])
+    return jnp.moveaxis(shard.reshape(*before, devices, -1, *after), dim, 0)
+
+
+def laid_out_2(parts, dim):
+    lengths = list(parts.shape[1:])
+    lengths[dim] *= parts.shape[0]
+    return jnp.moveaxis(parts, 0, dim).reshape(lengths)
 
 
 def laid_out(tiles, dim):
@@ -122,7 +133,14 @@
         jnp.bfloat16
     )
     back_rows = return_slots(results, starts_in, kept_in, slot_count)
-    returned = lax.all_to_all(back_rows, "attn", split_axis=0, concat_axis=0, tiled=True)
+    length, index = (lax.axis_size("attn"), lax.axis_index("attn"))
+    blocks = cut_along(back_rows, 0, length)
+    finished = [blocks[index]]
+    for lap in range(1, length):
+        sent = blocks[index ^ lap]
+        finished.append(lax.ppermute(sent, "attn", [(i, i ^ lap) for i in range(length)]))
+    blocks = jnp.stack(finished)[index ^ jnp.arange(length)]
+    returned = laid_out_2(blocks, 0)
     slot_of = jnp.take_along_axis(local_rank, expert_ids, axis=1)
     place_of = jnp.take_along_axis(position, expert_ids, axis=1)
     keep_mask = place_of < capacity

time: 320 us -> 359 us (1.12)
  starting transfers between devices: 20 us -> 54.6 us
  local copies, waits for them, and re-layouts: 96.5 us -> 118 us
  waiting for transfers between devices: 134 us -> 117 us
    ppermute x0 -> x15, waiting for transfers between devices: none -> 55.2 us  [body(): lax.ppermute(sent, 'attn', [(i, i ^ lap) for i in range(length)])]
    all_to_all x1 -> x0, waiting for transfers between devices: 47.5 us -> none  [body(): lax.all_to_all(back_rows, 'attn', split_axis=0, concat_axis=0, tiled=True)]
    ppermute x0 -> x15, starting transfers between devices: none -> 44.7 us  [body(): lax.ppermute(sent, 'attn', [(i, i ^ lap) for i in range(length)])]
    all_to_all x2, waiting for transfers between devices: 40.9 us -> 18.5 us  [copy_for_each(): lax.all_to_all(jnp.broadcast_to(shard[None], (count, *shard.shape)), axis...]
    unnamed x22 -> x41, local copies, waits for them, and re-layouts: 5.01 us -> 17.8 us
    all_to_all x1 -> x0, starting transfers between devices: 9.88 us -> none  [body(): lax.all_to_all(back_rows, 'attn', split_axis=0, concat_axis=0, tiled=True)]
    gather x0 -> x1, local copies, waits for them, and re-layouts: none -> 4.3 us  [body(): blocks = jnp.stack(finished)[index ^ jnp.arange(length)]]
  transfers between devices with their start and end apart: 4 -> 18, of which waited for: 4 -> 12; matrix products, arithmetic and copies ran while one was open for 22% -> 22% of each run, Pallas kernels for 0% -> 0%
where the time goes in v1:
time: 359 us; the launch traced here: 358 us
  local copies, waits for them, and re-layouts  118 us (33%)
  waiting for transfers between devices  117 us (33%)
  starting transfers between devices  54.6 us (15%)
  blocking collectives  30.9 us (9%)
  between operations  14.4 us (4%)
  other arithmetic  14.1 us (4%)
  matrix products  8.71 us (2%)
    ppermute x15, waiting for transfers between devices, body(): lax.ppermute(sent, 'attn', [(i, i ^ lap) for i in range(length)])  55.2 us
    ppermute x15, starting transfers between devices, body(): lax.ppermute(sent, 'attn', [(i, i ^ lap) for i in range(length)])  44.7 us
    reduce_scatter x1, waiting for transfers between devices, body(): lax.psum_scatter(both_parts.astype(jnp.bfloat16), 'expert', scatter_dimen...  43.4 us
    all_to_all x1, blocking collectives, copy_for_each(): lax.all_to_all(jnp.broadcast_to(shard[None], (count, *shard.shape)), axis...  30.9 us
    scatter x1, local copies, waits for them, and re-layouts, body(): pack_index = jnp.full((local_experts * capacity,), all_rows, jnp.int32).a...  30.4 us
    all_to_all x2, waiting for transfers between devices, copy_for_each(): lax.all_to_all(jnp.broadcast_to(shard[None], (count, *shard.shape)), axis...  18.5 us
    unnamed x41, local copies, waits for them, and re-layouts  17.8 us
    gather x1, local copies, waits for them, and re-layouts, return_slots(): return pad_rows(results)[row_index]  14.7 us
  transfers between devices with their start and end apart: 18, of which 12 were waited for; matrix products, arithmetic and copies ran while one was open for 22% of the time, Pallas kernels for 0%

profile of v1, /device:TPU:513, one launch (start us, length us, event | category | flops | bytes accessed | tf_op | source)
XLA Modules:
  0.0 357.7 jit_solution(14303782796586033204)
XLA Ops:
  8.0 30.9 %all_to_all.15 = s32[16,128,8]{1,2,0:T(8,128)S(1)} all-to-all(s32[16,128,8]{1,2,0:T(8,128)S(1)} %broadcast_in_dim.36), channel_id=1, replica_groups=mesh['groups'=2,'attn'=16,'expert'=8] {'attn'}, dimensions={0} | all-to-all | bytes 131072 | tf_op jit(solution)/shard_map/all_to_all | solution.py:26
  38.9 2.5 broadcast_in_dim.39
  41.4 4.5 %all-to-all-start.1 = ((bf16[16,128,512]{2,1,0:T(8,128)(2,1)}), bf16[16,128,512]{2,1,0:T(8,128)(2,1)}, u32[]{:S(2)}, u32[]{:S(2)}) async-start(bf16[16,128,512]{2,1,0:T(8,128)(2,1)} %broadcast_in_dim.39), calls=%async_computation.1 | async-start | bytes 4194304 | tf_op jit(solution)/shard_map/all_to_all | solution.py:26
  57.2 30.4 %scatter_custom_fusion = s32[1024]{0:T(1024)S(1)} fusion(s32[8192]{0:T(1024)S(1)} %bitcast.109, s32[8192]{0:T(1024)S(1)} %reshape.251, s32[]{:T(128)} %constant.49.clone.1), kind=kCustom, calls=%fused_computation.93 | custom fusion | bytes 4100 | tf_op jit(solution)/shard_map/scatter | solution.py:119
  87.6 7.5 %all-to-all-done.1 = bf16[16,128,512]{2,1,0:T(8,128)(2,1)} async-done(((bf16[16,128,512]{2,1,0:T(8,128)(2,1)}), bf16[16,128,512]{2,1,0:T(8,128)(2,1)}, u32[]{:S(2)}, u32[]{:S(2)}) %all-to-all-start.1) | async-done | bytes 2097184 | tf_op jit(solution)/shard_map/all_to_all | solution.py:26
  95.2 3.1 concatenate.10
  98.3 7.0 %gather_fusion = bf16[1024,512]{1,0:T(8,128)(2,1)} fusion(bf16[2049,512]{1,0:T(8,128)(2,1)} %concatenate.10, s32[1024]{0:T(1024)S(1)} %fusion.22), kind=kCustom, calls=%fused_computation.2 | custom fusion | bytes 2101248 | tf_op jit(solution)/shard_map/gather | solution.py:121
  105.3 2.4 convolution_convert_fusion
  112.4 43.4 %reduce-scatter.2.cloned.1.call-done = bf16[4,32,1536]{2,1,0:T(8,128)(2,1)} async-done(((bf16[4,256,1536]{2,1,0:T(8,128)(2,1)}), bf16[4,32,1536]{2,1,0:T(8,128)(2,1)}) %reduce-scatter.2.cloned.1.call-update) | async-done | bytes 393232 | tf_op jit(solution)/shard_map/reduce_scatter | solution.py:125
  158.3 5.3 %all-to-all-start.2 = ((bf16[8,4,32,768]{3,2,1,0:T(8,128)(2,1)}), bf16[8,4,32,768]{3,2,1,0:T(8,128)(2,1)}, u32[]{:S(2)}, u32[]{:S(2)}) async-start(bf16[8,4,32,768]{3,2,1,0:T(8,128)(2,1)} %broadcast_in_dim.44), calls=%async_computation.3 | async-start | bytes 3145728 | tf_op jit(solution)/shard_map/all_to_all | solution.py:26
  166.2 2.5 fusion.15
  175.4 7.1 %gather_fusion.5 = s32[1024]{0:T(1024)S(1)} fusion(s32[128,64]{1,0:T(8,128)S(1)} %get-tuple-element.4, s32[1024]{0:T(1024)S(1)} %reshape.272), kind=kCustom, calls=%fused_computation.1.clone | custom fusion | bytes 16384 | tf_op jit(solution)/shard_map/jit(take_along_axis)/gather | solution.py:144
  182.9 7.1 %gather_fusion.4 = s32[1024]{0:T(1024)S(1)} fusion(s32[128,64]{1,0:T(8,128)S(1)} %get-tuple-element.3, s32[1024]{0:T(1024)S(1)} %reshape.272), kind=kCustom, calls=%fused_computation.clone | custom fusion | bytes 16384 | tf_op jit(solution)/shard_map/jit(take_along_axis)/gather | solution.py:145
  190.1 10.9 %all-to-all-done.2 = bf16[8,4,32,768]{3,2,1,0:T(8,128)(2,1)} async-done(((bf16[8,4,32,768]{3,2,1,0:T(8,128)(2,1)}), bf16[8,4,32,768]{3,2,1,0:T(8,128)(2,1)}, u32[]{:S(2)}, u32[]{:S(2)}) %all-to-all-start.2) | async-done | bytes 1572896 | tf_op jit(solution)/shard_map/all_to_all | solution.py:26
  205.4 14.7 %gather_fusion.1 = bf16[3072,512]{1,0:T(8,128)(2,1)} fusion(bf16[1025,512]{1,0:T(8,128)(2,1)} %concatenate.12, s32[3072]{0:T(1024)S(1)} %broadcast_clamp_fusion), kind=kCustom, calls=%fused_computation.3 | custom fusion | bytes 6303744 | tf_op jit(solution)/shard_map/gather | solution.py:53
  220.1 3.5 constant_dynamic-slice_fusion
  223.6 3.8 %collective-permute-start = (bf16[1,4,48,512]{3,2,1,0:T(8,128)(2,1)}, bf16[1,4,48,512]{3,2,1,0:T(8,128)(2,1)}, u32[]{:S(2)}, u32[]{:S(2)}) collective-permute-start(bf16[1,4,48,512]{3,2,1,0:T(8,128)(2,1)} %get-tuple-element.19), channel_id=1, source_target_pairs={{0,8},{8,0},{16,24},{24,16},{32,40},{40,32},{48,56},{56,48},{64,72... | collective-permute-start | bytes 589832 | tf_op jit(solution)/shard_map/ppermute | solution.py:141
  233.7 3.5 collective-permute-start.5
  238.8 3.3 collective-permute-done.1
  242.1 2.5 collective-permute-start.6
  246.5 4.0 %collective-permute-start.7 = (bf16[1,4,48,512]{3,2,1,0:T(8,128)(2,1)}, bf16[1,4,48,512]{3,2,1,0:T(8,128)(2,1)S(1)}, u32[]{:S(2)}, u32[]{:S(2)}) collective-permute-start(bf16[1,4,48,512]{3,2,1,0:T(8,128)(2,1)} %get-tuple-element.12), channel_id=1, source_target_pairs={{0,64},{8,72},{16,80},{24,88},{32,96},{40,104},{48,112},{56,120},{... | collective-permute-start | bytes 589832 | tf_op jit(solution)/shard_map/ppermute | solution.py:141
  253.6 16.6 %collective-permute-done.4 = bf16[1,4,48,512]{3,2,1,0:T(8,128)(2,1)S(1)} collective-permute-done((bf16[1,4,48,512]{3,2,1,0:T(8,128)(2,1)}, bf16[1,4,48,512]{3,2,1,0:T(8,128)(2,1)S(1)}, u32[]{:S(2)}, u32[]{:S(2)}) %collective-permute-start.4) | collective-permute-done | bytes 196640 | tf_op jit(solution)/shard_map/ppermute | solution.py:141
  270.9 18.3 %collective-permute-start.10 = (bf16[1,4,48,512]{3,2,1,0:T(8,128)(2,1)}, bf16[1,4,48,512]{3,2,1,0:T(8,128)(2,1)S(1)}, u32[]{:S(2)}, u32[]{:S(2)}) collective-permute-start(bf16[1,4,48,512]{3,2,1,0:T(8,128)(2,1)} %get-tuple-element.9), channel_id=1, source_target_pairs={{0,88},{8,80},{16,72},{24,64},{32,120},{40,112},{48,104},{56,96},{... | collective-permute-start | bytes 589832 | tf_op jit(solution)/shard_map/ppermute | solution.py:141
  295.5 3.2 collective-permute-start.14
  299.4 17.5 %collective-permute-done.10 = bf16[1,4,48,512]{3,2,1,0:T(8,128)(2,1)S(1)} collective-permute-done((bf16[1,4,48,512]{3,2,1,0:T(8,128)(2,1)}, bf16[1,4,48,512]{3,2,1,0:T(8,128)(2,1)S(1)}, u32[]{:S(2)}, u32[]{:S(2)}) %collective-permute-start.10) | collective-permute-done | bytes 196640 | tf_op jit(solution)/shard_map/ppermute | solution.py:141
  317.6 3.5 collective-permute-done.11
  321.8 3.4 collective-permute-done.12
  325.9 6.4 %collective-permute-done.13 = bf16[1,4,48,512]{3,2,1,0:T(8,128)(2,1)S(1)} collective-permute-done((bf16[1,4,48,512]{3,2,1,0:T(8,128)(2,1)S(1)}, bf16[1,4,48,512]{3,2,1,0:T(8,128)(2,1)S(1)}, u32[]{:S(2)}, u32[]{:S(2)}) %collective-permute-start.13) | collective-permute-done | bytes 196640 | tf_op jit(solution)/shard_map/ppermute | solution.py:141
  333.1 2.8 collective-permute-done.14
  336.6 4.3 %gather_fusion.2 = bf16[16,4,48,512]{3,2,1,0:T(8,128)(2,1)} fusion(bf16[16,4,48,512]{3,2,1,0:T(8,128)(2,1)} %bitcast.28, s32[1024]{0:T(1024)S(1)} %pad_clamp_fusion), kind=kCustom, calls=%fused_computation.4 | custom fusion | bytes 6291520 | tf_op jit(solution)/shard_map/gather | solution.py:142
  340.9 7.4 %gather_fusion.3 = bf16[1024,512]{1,0:T(8,128)(2,1)} fusion(bf16[3072,512]{1,0:T(8,128)(2,1)} %bitcast.97, s32[1024]{0:T(1024)S(1)} %broadcast_clamp_fusion.1), kind=kCustom, calls=%fused_computation.5 | custom fusion | bytes 2101248 | tf_op jit(solution)/shard_map/gather | solution.py:147
  348.3 2.6 fusion.2
  (116 shorter events, 57.6 us)
Async XLA Ops:
  7.2 98.1 %copy-start = (bf16[4,512,768]{2,1,0:T(8,128)(2,1)S(1)}, bf16[4,512,768]{2,1,0:T(8,128)(2,1)}, u32[]{:S(2)}) copy-start(bf16[4,512,768]{2,1,0:T(8,128)(2,1)} %param.16) | copy-start | bytes 9437188
  41.4 53.8 %all-to-all-start.1 = ((bf16[16,128,512]{2,1,0:T(8,128)(2,1)}), bf16[16,128,512]{2,1,0:T(8,128)(2,1)}, u32[]{:S(2)}, u32[]{:S(2)}) async-start(bf16[16,128,512]{2,1,0:T(8,128)(2,1)} %broadcast_in_dim.39), calls=%async_computation.1 | async-start | bytes 4194304 | tf_op jit(solution)/shard_map/all_to_all | solution.py:26
  45.9 109.9 %reduce-scatter.2.cloned.1.call-start = ((), (), s32[]{:S(2)}) async-start(), calls=%async_computation.4 | async-start | bytes 3538944 | tf_op jit(solution)/shard_map/reduce_scatter | solution.py:125
  50.4 0.8 copy-start.3
  105.3 2.4 copy-start.1
  105.3 2.5 copy-start.2
  110.7 0.7 copy-start.7
  111.6 46.7 %copy-start.6 = (pred[128,64]{1,0:T(8,128)(4,1)}, pred[128,64]{1,0:T(8,128)(4,1)S(1)}, u32[]{:S(2)}) copy-start(pred[128,64]{1,0:T(8,128)(4,1)S(1)} %copy.126) | copy-start | bytes 24580
  156.9 7.0 %copy-start.9 = (s32[2]{0:T(128)S(1)}, s32[2]{0:T(128)}, u32[]{:S(2)}) copy-start(s32[2]{0:T(128)} %param.21) | copy-start | bytes 28
  158.3 42.7 %all-to-all-start.2 = ((bf16[8,4,32,768]{3,2,1,0:T(8,128)(2,1)}), bf16[8,4,32,768]{3,2,1,0:T(8,128)(2,1)}, u32[]{:S(2)}, u32[]{:S(2)}) async-start(bf16[8,4,32,768]{3,2,1,0:T(8,128)(2,1)} %broadcast_in_dim.44), calls=%async_computation.3 | async-start | bytes 3145728 | tf_op jit(solution)/shard_map/all_to_all | solution.py:26
  182.8 7.2 %copy-start.8 = (bf16[128,8]{0,1:T(8,128)(2,1)S(1)}, bf16[128,8]{0,1:T(8,128)(2,1)}, u32[]{:S(2)}) copy-start(bf16[128,8]{0,1:T(8,128)(2,1)} %param.14) | copy-start | bytes 6148
  201.0 2.4 copy-start.10
  223.6 10.1 %collective-permute-start = (bf16[1,4,48,512]{3,2,1,0:T(8,128)(2,1)}, bf16[1,4,48,512]{3,2,1,0:T(8,128)(2,1)}, u32[]{:S(2)}, u32[]{:S(2)}) collective-permute-start(bf16[1,4,48,512]{3,2,1,0:T(8,128)(2,1)} %get-tuple-element.19), channel_id=1, source_target_pairs={{0,8},{8,0},{16,24},{24,16},{32,40},{40,32},{48,56},{56,48},{64,72... | collective-permute-start | bytes 589832 | tf_op jit(solution)/shard_map/ppermute | solution.py:141
  227.4 64.4 %copy-start.5 = (bf16[1,4,48,512]{3,2,1,0:T(8,128)(2,1)S(1)}, bf16[1,4,48,512]{3,2,1,0:T(8,128)(2,1)}, u32[]{:S(2)}) copy-start(bf16[1,4,48,512]{3,2,1,0:T(8,128)(2,1)} %get-tuple-element.7) | copy-start | bytes 589828
  227.5 66.3 %copy-start.4 = (bf16[1,4,48,512]{3,2,1,0:T(8,128)(2,1)S(1)}, bf16[1,4,48,512]{3,2,1,0:T(8,128)(2,1)}, u32[]{:S(2)}) copy-start(bf16[1,4,48,512]{3,2,1,0:T(8,128)(2,1)} %get-tuple-element.6) | copy-start | bytes 589828
  227.5 14.6 %collective-permute-start.1 = (bf16[1,4,48,512]{3,2,1,0:T(8,128)(2,1)}, bf16[1,4,48,512]{3,2,1,0:T(8,128)(2,1)S(1)}, u32[]{:S(2)}, u32[]{:S(2)}) collective-permute-start(bf16[1,4,48,512]{3,2,1,0:T(8,128)(2,1)} %get-tuple-element.18), channel_id=1, source_target_pairs={{0,16},{8,24},{16,0},{24,8},{32,48},{40,56},{48,32},{56,40},{64,80... | collective-permute-start | bytes 589832 | tf_op jit(solution)/shard_map/ppermute | solution.py:141
  229.0 17.5 %collective-permute-start.2 = (bf16[1,4,48,512]{3,2,1,0:T(8,128)(2,1)}, bf16[1,4,48,512]{3,2,1,0:T(8,128)(2,1)S(1)}, u32[]{:S(2)}, u32[]{:S(2)}) collective-permute-start(bf16[1,4,48,512]{3,2,1,0:T(8,128)(2,1)} %get-tuple-element.17), channel_id=1, source_target_pairs={{0,24},{8,16},{16,8},{24,0},{32,56},{40,48},{48,40},{56,32},{64,88... | collective-permute-start | bytes 589832 | tf_op jit(solution)/shard_map/ppermute | solution.py:141
  229.3 21.9 %collective-permute-start.3 = (bf16[1,4,48,512]{3,2,1,0:T(8,128)(2,1)}, bf16[1,4,48,512]{3,2,1,0:T(8,128)(2,1)S(1)}, u32[]{:S(2)}, u32[]{:S(2)}) collective-permute-start(bf16[1,4,48,512]{3,2,1,0:T(8,128)(2,1)} %get-tuple-element.16), channel_id=1, source_target_pairs={{0,32},{8,40},{16,48},{24,56},{32,0},{40,8},{48,16},{56,24},{64,96... | collective-permute-start | bytes 589832 | tf_op jit(solution)/shard_map/ppermute | solution.py:141
  231.5 38.7 %collective-permute-start.4 = (bf16[1,4,48,512]{3,2,1,0:T(8,128)(2,1)}, bf16[1,4,48,512]{3,2,1,0:T(8,128)(2,1)S(1)}, u32[]{:S(2)}, u32[]{:S(2)}) collective-permute-start(bf16[1,4,48,512]{3,2,1,0:T(8,128)(2,1)} %get-tuple-element.15), channel_id=1, source_target_pairs={{0,40},{8,32},{16,56},{24,48},{32,8},{40,0},{48,24},{56,16},{64,10... | collective-permute-start | bytes 589832 | tf_op jit(solution)/shard_map/ppermute | solution.py:141
  233.7 37.2 %collective-permute-start.5 = (bf16[1,4,48,512]{3,2,1,0:T(8,128)(2,1)}, bf16[1,4,48,512]{3,2,1,0:T(8,128)(2,1)S(1)}, u32[]{:S(2)}, u32[]{:S(2)}) collective-permute-start(bf16[1,4,48,512]{3,2,1,0:T(8,128)(2,1)} %get-tuple-element.14), channel_id=1, source_target_pairs={{0,48},{8,56},{16,32},{24,40},{32,16},{40,24},{48,0},{56,8},{64,11... | collective-permute-start | bytes 589832 | tf_op jit(solution)/shard_map/ppermute | solution.py:141
  242.1 47.8 %collective-permute-start.6 = (bf16[1,4,48,512]{3,2,1,0:T(8,128)(2,1)}, bf16[1,4,48,512]{3,2,1,0:T(8,128)(2,1)S(1)}, u32[]{:S(2)}, u32[]{:S(2)}) collective-permute-start(bf16[1,4,48,512]{3,2,1,0:T(8,128)(2,1)} %get-tuple-element.13), channel_id=1, source_target_pairs={{0,56},{8,48},{16,40},{24,32},{32,24},{40,16},{48,8},{56,0},{64,12... | collective-permute-start | bytes 589832 | tf_op jit(solution)/shard_map/ppermute | solution.py:141
  246.5 45.4 %collective-permute-start.7 = (bf16[1,4,48,512]{3,2,1,0:T(8,128)(2,1)}, bf16[1,4,48,512]{3,2,1,0:T(8,128)(2,1)S(1)}, u32[]{:S(2)}, u32[]{:S(2)}) collective-permute-start(bf16[1,4,48,512]{3,2,1,0:T(8,128)(2,1)} %get-tuple-element.12), channel_id=1, source_target_pairs={{0,64},{8,72},{16,80},{24,88},{32,96},{40,104},{48,112},{56,120},{... | collective-permute-start | bytes 589832 | tf_op jit(solution)/shard_map/ppermute | solution.py:141
  251.2 42.6 %collective-permute-start.8 = (bf16[1,4,48,512]{3,2,1,0:T(8,128)(2,1)}, bf16[1,4,48,512]{3,2,1,0:T(8,128)(2,1)S(1)}, u32[]{:S(2)}, u32[]{:S(2)}) collective-permute-start(bf16[1,4,48,512]{3,2,1,0:T(8,128)(2,1)} %get-tuple-element.11), channel_id=1, source_target_pairs={{0,72},{8,64},{16,88},{24,80},{32,104},{40,96},{48,120},{56,112},{... | collective-permute-start | bytes 589832 | tf_op jit(solution)/shard_map/ppermute | solution.py:141
  270.2 25.3 %collective-permute-start.9 = (bf16[1,4,48,512]{3,2,1,0:T(8,128)(2,1)}, bf16[1,4,48,512]{3,2,1,0:T(8,128)(2,1)S(1)}, u32[]{:S(2)}, u32[]{:S(2)}) collective-permute-start(bf16[1,4,48,512]{3,2,1,0:T(8,128)(2,1)} %get-tuple-element.10), channel_id=1, source_target_pairs={{0,80},{8,88},{16,64},{24,72},{32,112},{40,120},{48,96},{56,104},{... | collective-permute-start | bytes 589832 | tf_op jit(solution)/shard_map/ppermute | solution.py:141
  270.9 46.0 %collective-permute-start.10 = (bf16[1,4,48,512]{3,2,1,0:T(8,128)(2,1)}, bf16[1,4,48,512]{3,2,1,0:T(8,128)(2,1)S(1)}, u32[]{:S(2)}, u32[]{:S(2)}) collective-permute-start(bf16[1,4,48,512]{3,2,1,0:T(8,128)(2,1)} %get-tuple-element.9), channel_id=1, source_target_pairs={{0,88},{8,80},{16,72},{24,64},{32,120},{40,112},{48,104},{56,96},{... | collective-permute-start | bytes 589832 | tf_op jit(solution)/shard_map/ppermute | solution.py:141
  289.8 31.3 %collective-permute-start.11 = (bf16[1,4,48,512]{3,2,1,0:T(8,128)(2,1)}, bf16[1,4,48,512]{3,2,1,0:T(8,128)(2,1)S(1)}, u32[]{:S(2)}, u32[]{:S(2)}) collective-permute-start(bf16[1,4,48,512]{3,2,1,0:T(8,128)(2,1)} %get-tuple-element.8), channel_id=1, source_target_pairs={{0,96},{8,104},{16,112},{24,120},{32,64},{40,72},{48,80},{56,88},{... | collective-permute-start | bytes 589832 | tf_op jit(solution)/shard_map/ppermute | solution.py:141
  291.9 33.3 %collective-permute-start.12 = (bf16[1,4,48,512]{3,2,1,0:T(8,128)(2,1)S(1)}, bf16[1,4,48,512]{3,2,1,0:T(8,128)(2,1)S(1)}, u32[]{:S(2)}, u32[]{:S(2)}) collective-permute-start(bf16[1,4,48,512]{3,2,1,0:T(8,128)(2,1)S(1)} %copy-done.5), channel_id=1, source_target_pairs={{0,104},{8,96},{16,120},{24,112},{32,72},{40,64},{48,88},{56,80},{... | collective-permute-start | bytes 589832 | tf_op jit(solution)/shard_map/ppermute | solution.py:141
  293.8 38.6 %collective-permute-start.13 = (bf16[1,4,48,512]{3,2,1,0:T(8,128)(2,1)S(1)}, bf16[1,4,48,512]{3,2,1,0:T(8,128)(2,1)S(1)}, u32[]{:S(2)}, u32[]{:S(2)}) collective-permute-start(bf16[1,4,48,512]{3,2,1,0:T(8,128)(2,1)S(1)} %copy-done.4), channel_id=1, source_target_pairs={{0,112},{8,120},{16,96},{24,104},{32,80},{40,88},{48,64},{56,72},{... | collective-permute-start | bytes 589832 | tf_op jit(solution)/shard_map/ppermute | solution.py:141
  295.5 40.3 %collective-permute-start.14 = (bf16[1,4,48,512]{3,2,1,0:T(8,128)(2,1)S(1)}, bf16[1,4,48,512]{3,2,1,0:T(8,128)(2,1)S(1)}, u32[]{:S(2)}, u32[]{:S(2)}) collective-permute-start(bf16[1,4,48,512]{3,2,1,0:T(8,128)(2,1)S(1)} %get-tuple-element.5), channel_id=1, source_target_pairs={{0,120},{8,112},{16,104},{24,96},{32,88},{40,80},{48,72},{56,64},{... | collective-permute-start | bytes 589832 | tf_op jit(solution)/shard_map/ppermute | solution.py:141
Sparse Core Ops, SparseCore 0:
  110.9 44.8 reduce-scatter.1
